TPU v7x, 32 devices: a whole 2x2x4 slice. The times are simulated.
32 devices in a mesh: member: 4 (over y, x), region: 2 (over core), block: 4 (over z).
Axes of the slice: x: 2, y: 2, z: 4, core: 2. Of those that a mesh axis runs over, the one named last changes fastest.
Arguments:
- traffic_load: float32 [128, 65536], P('member', ('region', 'block')), may hold values from 0.05 to 0.7
- free_speed: float32 [65536], P(('region', 'block')), may hold values from 0.3 to 0.95
- wave_speed: float32 [65536], P(('region', 'block')), may hold values from 0.15 to 0.6
- jam_density: float32 [65536], P(('region', 'block')), may hold values from 0.8 to 1.2
- capacity_share: float32 [65536], P(('region', 'block')), may hold values from 0.5 to 1
- observation_cell: int32 [24576], P(('region', 'block')), may hold values from 0 to 2047
- obs_count: int32 [32], P(('region', 'block')), may hold values from 1 to 768, 12288 in all
- observation_value: float32 [24576], P(('region', 'block')), may hold values from 0 to 0.8
- observation_variance: float32 [24576], P(('region', 'block')), may hold values from 0.002 to 0.02
- observation_noise: float32 [128, 24576], P('member', ('region', 'block')), may hold values from -6 to 6
- block_lists: int32 [32, 3], P(('region', 'block')), may hold values from 0 to 31, as said below
Outputs:
- analysis: float32 [128, 65536], P('member', ('region', 'block'))
Inputs may be any that keep to these rules, and one draw needn't show every extreme that they name: `block_lists`: row b lists 3 different blocks, b itself among them, each within 4 blocks of b.
All inputs are finite; a program needn't handle non-finite values. No bound on the sum of `obs_count` on one device may be relied on, other than what follows from the above.
Results may differ from a plain program's by a relative error of at most 0.0003.
Values sent between devices are 32-bit elements; how exact they have to be, the bound alone decides.
A program may use at most 64 MiB of HBM per device.

v0:
```python
import jax
import jax.numpy as jnp
from jax import lax
from jax.sharding import PartitionSpec as P

REALIZATION_TALLY = 128
HORIZON_TICKS = 16
CELLS_PER_BLOCK = 2048
BLOCK_SLOTS = 768


def padded(value, sides, width):
    for axis, dim in sides:
        size, length = (lax.axis_size(axis), value.shape[dim])
        up = [(i, (i + 1) % size) for i in range(size - 1)]
        down = [(j, i) for i, j in up]
        last = lax.slice_in_dim(value, length - width, length, axis=dim)
        leading = lax.slice_in_dim(value, 0, width, axis=dim)
        before = lax.ppermute(last, axis, up)
        after = lax.ppermute(leading, axis, down)
        value = jnp.concatenate([before, value, after], axis=dim)
    return value


def road_capacity(free_speed, wave_speed, jam_density, capacity_share):
    return capacity_share * free_speed * wave_speed * jam_density / (free_speed + wave_speed)


def block_products(left_side, right_side, weight, block_total):
    member_count = left_side.shape[0]
    left_blocks = (left_side * weight).reshape(member_count, block_total, -1)
    right_blocks = right_side.reshape(member_count, block_total, -1)
    return jnp.einsum("kbo,jbo->bkj", left_blocks, right_blocks, precision=lax.Precision.HIGHEST)


def body(
    traffic_load,
    free_speed,
    wave_speed,
    jam_density,
    capacity_share,
    observation_cell,
    obs_count,
    observation_value,
    observation_variance,
    observation_noise,
    block_lists,
):
    mem_local, cell_total = traffic_load.shape
    block_total = obs_count.shape[0]
    slot_total = observation_cell.shape[0]
    capacity = road_capacity(free_speed, wave_speed, jam_density, capacity_share)
    is_last = lax.axis_index(("region", "block")) == lax.axis_size(("region", "block")) - 1
    margin = HORIZON_TICKS
    state_wide = padded(traffic_load, ((("region", "block"), 1),), margin)
    road_wide = padded(
        jnp.stack([free_speed, wave_speed, jam_density, capacity]),
        ((("region", "block"), 1),),
        margin,
    )
    speed_wide = road_wide[0]
    wave_wide = road_wide[1]
    jam_wide = road_wide[2]
    capacity_wide = road_wide[3]
    exit_mask = (jnp.arange(cell_total + 2 * margin) == cell_total + margin) & is_last
    exit_value = capacity[-1]

    def advance_wide(step_index, state):
        demand = jnp.minimum(speed_wide * state, capacity_wide)
        supply = jnp.minimum(capacity_wide, wave_wide * (jam_wide - state))
        supply = jnp.where(exit_mask[None, :], exit_value, supply)
        fluxes = jnp.minimum(demand[:, :-1], supply[:, 1:])
        updated = state[:, 1:-1] + fluxes[:, :-1] - fluxes[:, 1:]
        return state.at[:, 1:-1].set(updated)

    predicted_traffic_load = lax.fori_loop(0, HORIZON_TICKS, advance_wide, state_wide)[
        :, margin : margin + cell_total
    ]
    realization_total = lax.psum(jnp.sum(predicted_traffic_load, axis=0), "member")
    realization_average = realization_total / REALIZATION_TALLY
    realization_departure = predicted_traffic_load - realization_average
    slot_cell_index = (
        jnp.arange(slot_total, dtype=jnp.int32) // BLOCK_SLOTS * CELLS_PER_BLOCK + observation_cell
    )
    obs_anomaly = jnp.take(realization_departure, slot_cell_index, axis=1)
    obs_mean = jnp.take(realization_average, slot_cell_index)
    live_mask = (
        (jnp.arange(BLOCK_SLOTS, dtype=jnp.int32)[None, :] < obs_count[:, None])
        .reshape(-1)
        .astype(jnp.float32)
    )
    weight = live_mask / observation_variance
    misfit = observation_value - obs_mean
    obs_all, noise_all = (
        lax.all_gather(obs_anomaly, "member", axis=0, tiled=True),
        lax.all_gather(observation_noise, "member", axis=0, tiled=True),
    )
    spread = jnp.sum(obs_all * obs_all, axis=0) / (REALIZATION_TALLY - 1)
    misfit_sum, spread_sum = lax.psum(
        (
            jnp.sum(misfit * misfit * weight),
            jnp.sum(live_mask * (spread / observation_variance + 1.0)),
        ),
        ("region", "block"),
    )
    inflation = jnp.sqrt(misfit_sum / spread_sum)
    perturbed = misfit + jnp.sqrt(observation_variance) * noise_all
    scaled = inflation * obs_all
    gram_part = block_products(scaled, scaled, weight, block_total)
    cross_part = block_products(scaled, perturbed - scaled, weight, block_total)
    neighbour_pairs = padded(
        jnp.stack([gram_part, cross_part]), ((("region", "block"), 1),), block_total
    )
    first_block = (lax.axis_index(("region", "block")) - 1) * block_total
    relative = block_lists - first_block
    selector = jnp.sum(
        (
            relative[:, :, None] == jnp.arange(3 * block_total, dtype=jnp.int32)[None, None, :]
        ).astype(jnp.float32),
        axis=1,
    )
    local_gram = jnp.einsum(
        "be,ekj->bkj", selector, neighbour_pairs[0], precision=lax.Precision.HIGHEST
    )
    local_cross = jnp.einsum(
        "be,ekj->bkj", selector, neighbour_pairs[1], precision=lax.Precision.HIGHEST
    )
    identity = (REALIZATION_TALLY - 1) * jnp.eye(REALIZATION_TALLY, dtype=jnp.float32)[None]
    system = identity + local_gram
    factors = jnp.linalg.cholesky(system)
    mixing = jax.vmap(lambda factor, target: jax.scipy.linalg.cho_solve((factor, True), target))(
        factors, local_cross
    )
    member_start = lax.axis_index("member") * mem_local
    own_columns = lax.dynamic_slice_in_dim(mixing, member_start, mem_local, 2)
    row_piece = lax.all_gather(realization_departure, "member", axis=0, tiled=True)
    row_count = row_piece.shape[0]
    piece_blocks = row_piece.reshape(row_count, block_total, CELLS_PER_BLOCK)
    change = (
        jnp.zeros((mem_local, block_total, CELLS_PER_BLOCK), jnp.float32)
        + jnp.einsum("kbc,bkj->jbc", piece_blocks, own_columns, precision=lax.Precision.HIGHEST)
    ).reshape(mem_local, cell_total)
    return realization_average + inflation * realization_departure + inflation * change


def solution(mesh):
    placed = (
        P("member", ("region", "block")),
        P(("region", "block")),
        P(("region", "block")),
        P(("region", "block")),
        P(("region", "block")),
        P(("region", "block")),
        P(("region", "block")),
        P(("region", "block")),
        P(("region", "block")),
        P("member", ("region", "block")),
        P(("region", "block"), None),
    )
    return jax.shard_map(
        body,
        mesh=mesh,
        in_specs=placed,
        out_specs=P("member", ("region", "block")),
        check_vma=False,
    )
```

profile of v0, /device:TPU:0, one launch (start us, length us, event | category | flops | bytes accessed | tf_op | source)
XLA Modules:
  0.0 368.9 jit_solution(8760085229739747867)
XLA Ops:
  8.4 4.9 %collective-permute-start.2 = (f32[4,16]{1,0:T(4,128)S(1)}, f32[4,16]{1,0:T(4,128)S(1)}, u32[]{:S(2)}, u32[]{:S(2)}) collective-permute-start(f32[4,16]{1,0:T(4,128)S(1)} %get-tuple-element.210), channel_id=1, source_target_pairs={{0,1},{1,2},{2,3},{3,4},{4,5},{5,6},{6,7},{8,9},{9,10},{10,11},{11... | collective-permute-start | bytes 776 | tf_op jit(solution)/shard_map/ppermute | solution.py:19
  15.5 4.5 %collective-permute-start = (f32[32,16]{1,0:T(8,128)S(1)}, f32[32,16]{1,0:T(8,128)S(1)}, u32[]{:S(2)}, u32[]{:S(2)}) collective-permute-start(f32[32,16]{1,0:T(8,128)S(1)} %get-tuple-element.204), channel_id=1, source_target_pairs={{0,1},{1,2},{2,3},{3,4},{4,5},{5,6},{6,7},{8,9},{9,10},{10,11},{11... | collective-permute-start | bytes 6152 | tf_op jit(solution)/shard_map/ppermute | solution.py:19
  26.4 90.7 %while.15 = (s32[]{:T(128)}, f32[32,8224]{1,0:T(8,128)S(1)}, pred[]{:T(512)}, f32[1,8224]{1,0:T(1,128)S(1)}, f32[1,8224]{1,0:T(1,128)S(1)}, /*index=5*/f32[]{:T(...) while((s32[]{:T(128)}, f32[32,8224]{1,0:T(8,128)S(1)}, ...), condition=%wide.region_2.3_spmd.clone, body=%wide.region_1.0_spmd.clone.sunk | while | flops 2647714 | bytes 10195928 | solution.py:76
  28.1 1.3 fusion.48
  29.4 2.7 scatter.7
  33.8 1.3 fusion.48
  35.1 2.7 scatter.7
  39.5 1.3 fusion.48
  40.8 2.7 scatter.7
  45.1 1.3 fusion.48
  46.4 2.7 scatter.7
  50.8 1.3 fusion.48
  52.1 2.7 scatter.7
  56.5 1.3 fusion.48
  57.8 2.7 scatter.7
  63.4 2.7 scatter.7
  69.1 2.7 scatter.7
  74.8 2.7 scatter.7
  79.1 1.3 fusion.48
  80.4 2.7 scatter.7
  86.1 2.7 scatter.7
  91.8 2.7 scatter.7
  97.4 2.7 scatter.7
  103.1 2.7 scatter.7
  108.8 2.7 scatter.7
  114.5 2.7 scatter.7
  117.5 16.3 %psum.21 = f32[8192]{0:T(1024)S(1)} all-reduce(f32[8192]{0:T(1024)S(1)} %slice_reduce_fusion), channel_id=1, replica_groups=mesh['member'=4,'region'=2,'block'=4] {'member'}, use_global_device_ids=true, to_apply=%region_4.5 | all-reduce | flops 8192 | bytes 65536 | tf_op jit(solution)/shard_map/psum | solution.py:79
  134.1 2.7 copy.79
  136.8 17.4 %gather_fusion = f32[3072]{0:T(1024)S(1)} fusion(f32[8192]{0:T(1024)S(1)} %broadcast_multiply_fusion.2, s32[3072]{0:T(1024)S(1)} %broadcast_clamp_fusion), kind=kCustom, calls=%fused_computation | custom fusion | bytes 36864 | tf_op jit(solution)/shard_map/jit(_take)/gather | solution.py:86
  154.3 13.0 %gather_fusion.1 = f32[3072,32]{1,0:T(8,128)} fusion(f32[32,8192]{0,1:T(8,128)} %copy.79, s32[3072]{0:T(1024)S(1)} %broadcast_clamp_fusion), kind=kCustom, calls=%fused_computation.1 | custom fusion | bytes 798720 | tf_op jit(solution)/shard_map/jit(_take)/gather | solution.py:85
  168.0 2.7 select_bitcast_fusion
  172.7 3.1 copy.85
  175.8 27.7 %all-gather.4.cloned.1.call-done = f32[128,3072]{1,0:T(8,128)} async-done(((f32[32,3072]{1,0:T(8,128)}), f32[128,3072]{1,0:T(8,128)}) %all-gather.4.cloned.1.call-update) | async-done | bytes 1572880 | tf_op jit(solution)/shard_map/all_gather | solution.py:95
  203.5 1.7 multiply_reduce_fusion
  205.9 17.1 %all-reduce = (f32[]{:T(128)}, f32[]{:T(128)}) all-reduce(f32[]{:T(128)} %get-tuple-element.195, f32[]{:T(128)} %select_reduce_fusion.1), channel_id=1, replica_groups=mesh['member'=4,'region'=2,'block'=4] {'region','block'}, use_global_device_ids=true, to_apply=%region_6.7 | all-reduce | flops 2 | bytes 16 | tf_op jit(solution)/shard_map/psum | solution.py:99
  224.3 1.6 copy.82
  226.0 3.2 add_subtract_fusion
  229.6 2.7 convolution_bitcast_fusion.1
  232.4 2.7 convolution_bitcast_fusion
  235.1 1.7 collective-permute-start.4
  236.8 1.5 collective-permute-start.5
  238.6 10.0 %collective-permute-done.4 = f32[2,4,128,128]{3,2,1,0:T(8,128)S(1)} collective-permute-done((f32[2,4,128,128]{3,2,1,0:T(8,128)S(1)}, f32[2,4,128,128]{3,2,1,0:T(8,128)S(1)}, u32[]{:S(2)}, u32[]{:S(2)}) %collective-permute-start.4) | collective-permute-done | bytes 524320 | tf_op jit(solution)/shard_map/ppermute | solution.py:19
  248.6 10.3 %collective-permute-done.5 = f32[2,4,128,128]{3,2,1,0:T(8,128)S(1)} collective-permute-done((f32[2,4,128,128]{3,2,1,0:T(8,128)S(1)}, f32[2,4,128,128]{3,2,1,0:T(8,128)S(1)}, u32[]{:S(2)}, u32[]{:S(2)}) %collective-permute-start.5) | collective-permute-done | bytes 524320 | tf_op jit(solution)/shard_map/ppermute | solution.py:20
  260.5 46.9 %custom-call.11 = f32[4,128,128]{2,1,0:T(8,128)S(1)} custom-call(f32[4,128,128]{2,1,0:T(8,128)S(1)} %fusion.19), custom_call_target="Cholesky" | custom-call | tf_op jit(solution)/shard_map/jit(cholesky)/cholesky | solution.py:130
  307.7 39.3 %custom-call.12 = f32[4,1,128,128]{2,3,1,0:T(8,128)S(1)} custom-call(f32[4,1,128,128]{3,2,1,0:T(8,128)S(1)} %select_bitcast_fusion.1), custom_call_target="InvertDiagBlocksLowerTriangular" | custom-call | tf_op jit(solution)/shard_map/vmap(jit(_cho_solve))/triangular_solve | solution.py:131
  349.4 5.6 %copy.96 = f32[128,8192]{0,1:T(8,128)} copy(f32[128,8192]{1,0:T(8,128)} %all-gather.8.cloned.1.call-done) | data formatting | bytes 8388608 | tf_op jit(solution)/shard_map/all_gather | solution.py:136
  355.0 6.0 %fusion.9 = f32[4,4,8,2048]{3,2,1,0:T(8,128)S(1)} fusion(f32[128,4,2048]{0,2,1:T(8,128)} %bitcast.50, f32[]{:T(128)S(6)} %sqrt.6, f32[4,128,128]{1,2,0:T(8,128)S(1)} %fusion.14, s32[]{:T(128)S(6)} %select_n.38), kind=kOutput, calls=%fused_computation.16 | convolution fusion | flops 402915328 | bytes 5308424 | tf_op jit(solution)/shard_map/kbc,bkj->jbc/dot_general | solution.py:141
  361.0 1.3 add_add_fusion
  (235 shorter events, 57.3 us)
Async XLA Ops:
  6.5 19.2 %copy-start.2 = (f32[32,8192]{1,0:T(8,128)S(1)}, f32[32,8192]{1,0:T(8,128)}, u32[]{:S(2)}) copy-start(f32[32,8192]{1,0:T(8,128)} %param.15) | copy-start | bytes 3145732
  6.5 166.2 %all-gather.6.cloned.1.call-start = ((), (), s32[]{:S(2)}) async-start(), calls=%async_computation.1 | async-start | bytes 1966080 | tf_op jit(solution)/shard_map/all_gather | solution.py:96
  8.4 15.8 %collective-permute-start.2 = (f32[4,16]{1,0:T(4,128)S(1)}, f32[4,16]{1,0:T(4,128)S(1)}, u32[]{:S(2)}, u32[]{:S(2)}) collective-permute-start(f32[4,16]{1,0:T(4,128)S(1)} %get-tuple-element.210), channel_id=1, source_target_pairs={{0,1},{1,2},{2,3},{3,4},{4,5},{5,6},{6,7},{8,9},{9,10},{10,11},{11... | collective-permute-start | bytes 776 | tf_op jit(solution)/shard_map/ppermute | solution.py:19
  13.4 10.8 %collective-permute-start.3 = (f32[4,16]{1,0:T(4,128)S(1)}, f32[4,16]{1,0:T(4,128)S(1)}, u32[]{:S(2)}, u32[]{:S(2)}) collective-permute-start(f32[4,16]{1,0:T(4,128)S(1)} %get-tuple-element.209), channel_id=1, source_target_pairs={{1,0},{2,1},{3,2},{4,3},{5,4},{6,5},{7,6},{9,8},{10,9},{11,10},{12... | collective-permute-start | bytes 776 | tf_op jit(solution)/shard_map/ppermute | solution.py:20
  15.5 9.0 %collective-permute-start = (f32[32,16]{1,0:T(8,128)S(1)}, f32[32,16]{1,0:T(8,128)S(1)}, u32[]{:S(2)}, u32[]{:S(2)}) collective-permute-start(f32[32,16]{1,0:T(8,128)S(1)} %get-tuple-element.204), channel_id=1, source_target_pairs={{0,1},{1,2},{2,3},{3,4},{4,5},{5,6},{6,7},{8,9},{9,10},{10,11},{11... | collective-permute-start | bytes 6152 | tf_op jit(solution)/shard_map/ppermute | solution.py:19
  20.1 5.6 %collective-permute-start.1 = (f32[32,16]{1,0:T(8,128)S(1)}, f32[32,16]{1,0:T(8,128)S(1)}, u32[]{:S(2)}, u32[]{:S(2)}) collective-permute-start(f32[32,16]{1,0:T(8,128)S(1)} %get-tuple-element.203), channel_id=1, source_target_pairs={{1,0},{2,1},{3,2},{4,3},{5,4},{6,5},{7,6},{9,8},{10,9},{11,10},{12... | collective-permute-start | bytes 6152 | tf_op jit(solution)/shard_map/ppermute | solution.py:20
  21.4 182.1 %all-gather.4.cloned.1.call-start = ((), (), s32[]{:S(2)}) async-start(), calls=%async_computation | async-start | bytes 1966080 | tf_op jit(solution)/shard_map/all_gather | solution.py:95
  134.1 2.7 copy-start
  154.2 13.0 %copy-start.3 = (f32[3072]{0:T(1024)S(1)}, f32[3072]{0:T(1024)}, u32[]{:S(2)}) copy-start(f32[3072]{0:T(1024)} %param.23) | copy-start | bytes 36868
  154.3 13.0 %copy-start.4 = (s32[3072]{0:T(1024)S(1)}, s32[3072]{0:T(1024)}, u32[]{:S(2)}) copy-start(s32[3072]{0:T(1024)} %param.20) | copy-start | bytes 36868
  154.3 13.0 %copy-start.5 = (f32[3072]{0:T(1024)S(1)}, f32[3072]{0:T(1024)}, u32[]{:S(2)}) copy-start(f32[3072]{0:T(1024)} %param.22) | copy-start | bytes 36868
  172.0 177.4 %all-gather.8.cloned.1.call-start = ((), (), s32[]{:S(2)}) async-start(), calls=%async_computation.2 | async-start | bytes 5242880 | tf_op jit(solution)/shard_map/all_gather | solution.py:136
  203.5 20.8 %copy-start.1 = (f32[128,3072]{1,0:T(8,128)S(1)}, f32[128,3072]{1,0:T(8,128)}, u32[]{:S(2)}) copy-start(f32[128,3072]{1,0:T(8,128)} %all-gather.4.cloned.1.call-done) | copy-start | bytes 4718596
  232.3 6.0 %copy-start.6 = (s32[4,3]{1,0:T(4,128)S(1)}, s32[4,3]{1,0:T(4,128)}, u32[]{:S(2)}) copy-start(s32[4,3]{1,0:T(4,128)} %param.25) | copy-start | bytes 148
  235.1 13.5 %collective-permute-start.4 = (f32[2,4,128,128]{3,2,1,0:T(8,128)S(1)}, f32[2,4,128,128]{3,2,1,0:T(8,128)S(1)}, u32[]{:S(2)}, u32[]{:S(2)}) collective-permute-start(f32[2,4,128,128]{3,2,1,0:T(8,128)S(1)} %pad_maximum_fusion.1), channel_id=1, source_target_pairs={{0,1},{1,2},{2,3},{3,4},{4,5},{5,6},{6,7},{8,9},{9,10},{10,11},{11... | collective-permute-start | bytes 1572872 | tf_op jit(solution)/shard_map/ppermute | solution.py:19
  236.8 22.2 %collective-permute-start.5 = (f32[2,4,128,128]{3,2,1,0:T(8,128)S(1)}, f32[2,4,128,128]{3,2,1,0:T(8,128)S(1)}, u32[]{:S(2)}, u32[]{:S(2)}) collective-permute-start(f32[2,4,128,128]{3,2,1,0:T(8,128)S(1)} %pad_maximum_fusion.1), channel_id=1, source_target_pairs={{1,0},{2,1},{3,2},{4,3},{5,4},{6,5},{7,6},{9,8},{10,9},{11,10},{12... | collective-permute-start | bytes 1572872 | tf_op jit(solution)/shard_map/ppermute | solution.py:20
Sparse Core Ops, SparseCore 0:
  21.5 33.1 all-gather.5
  172.1 31.4 all-gather.3
  205.4 52.5 all-gather.7
where the time goes:
time: 370 us; the launch traced here: 369 us
  other arithmetic  144 us (39%)
  local copies, waits for them, and re-layouts  95.2 us (26%)
  waiting for transfers between devices  50 us (14%)
  blocking collectives  33.4 us (9%)
  starting transfers between devices  15.3 us (4%)
  matrix products  14.8 us (4%)
  between operations  14.8 us (4%)
    another operation x4, other arithmetic, body(): factors = jnp.linalg.cholesky(system)  47.1 us
    scatter x16, local copies, waits for them, and re-layouts, advance_wide(): return state.at[:, 1:-1].set(updated)  42.5 us
    another operation x3, other arithmetic, body(): jax.scipy.linalg.cho_solve((factor, True), target)  39.4 us
    all_gather x1, waiting for transfers between devices, body(): lax.all_gather(obs_anomaly, 'member', axis=0, tiled=True)  27.7 us
    another operation x17, other arithmetic  21.6 us
    gather x1, local copies, waits for them, and re-layouts, body(): obs_mean = jnp.take(realization_average, slot_cell_index)  17.4 us
    psum x1, blocking collectives, body(): lax.psum((jnp.sum(misfit * misfit * weight), jnp.sum(live_mask * (spread...  17.1 us
    psum x1, blocking collectives, body(): lax.psum(jnp.sum(predicted_traffic_load, axis=0), 'member')  16.3 us
  transfers between devices with their start and end apart: 9, of which 4 were waited for; matrix products, arithmetic and copies ran while one was open for 65% of the time, Pallas kernels for 0%

commit v1 on v0

--- a/solution.py
+++ b/solution.py
@@ -7,6 +7,28 @@
 HORIZON_TICKS = 16
 CELLS_PER_BLOCK = 2048
 BLOCK_SLOTS = 768
+
+
+def laid_out(parts, dim):
+    dims = list(parts.shape[1:])
+    dims[dim] *= parts.shape[0]
+    return jnp.moveaxis(parts, 0, dim).reshape(dims)
+
+
+def collected_by_bits(x, axis):
+    length = lax.axis_size(axis)
+    parts = x[None]
+    for level in range(length.bit_length() - 1):
+        bit = 1 << level
+        theirs = lax.ppermute(parts, axis, [(i, i ^ bit) for i in range(length)])
+        both = jnp.stack([parts, theirs])
+        upper = lax.axis_index(axis) >> level & 1
+        parts = jnp.where(upper == 0, both, both[::-1]).reshape(-1, *x.shape)
+    return parts
+
+
+def collect(shard, axis, dim):
+    return laid_out(collected_by_bits(shard, axis), dim)
 
 
 def padded(value, sides, width):
@@ -92,7 +114,7 @@
     weight = live_mask / observation_variance
     misfit = observation_value - obs_mean
     obs_all, noise_all = (
-        lax.all_gather(obs_anomaly, "member", axis=0, tiled=True),
+        collect(obs_anomaly, "member", 0),
         lax.all_gather(observation_noise, "member", axis=0, tiled=True),
     )
     spread = jnp.sum(obs_all * obs_all, axis=0) / (REALIZATION_TALLY - 1)

time: 370 us -> 382 us (1.032)
  other arithmetic: 144 us -> 151 us
  local copies, waits for them, and re-layouts: 95.2 us -> 99.9 us
    ppermute x0 -> x2, waiting for transfers between devices: none -> 32.8 us  [collected_by_bits(): theirs = lax.ppermute(parts, axis, [(i, i ^ bit) for i in range(length)])]
    all_gather x1 -> x0, waiting for transfers between devices: 27.7 us -> none  [body(): lax.all_gather(obs_anomaly, 'member', axis=0, tiled=True)]
    another operation x17 -> x20, other arithmetic: 21.6 us -> 27.5 us
    all_gather x2 -> x0, local copies, waits for them, and re-layouts: 4.76 us -> none  [the longest x1 3.11 us: body(): lax.all_gather(observation_noise, 'member', axis=0, tiled=True)]
    ppermute x3, waiting for transfers between devices: 11.5 us -> 7.16 us  [padded(): after = lax.ppermute(leading, axis, down)]
  transfers between devices with their start and end apart: 9 -> 10, of which waited for: 4 -> 5; matrix products, arithmetic and copies ran while one was open for 65% -> 65% of each run, Pallas kernels for 0% -> 0%
where the time goes in v1:
time: 382 us; the launch traced here: 381 us
  other arithmetic  151 us (40%)
  local copies, waits for them, and re-layouts  99.9 us (26%)
  waiting for transfers between devices  50.7 us (13%)
  blocking collectives  30.8 us (8%)
  starting transfers between devices  18.6 us (5%)
  between operations  15.2 us (4%)
  matrix products  14.5 us (4%)
    another operation x4, other arithmetic, body(): factors = jnp.linalg.cholesky(system)  47.1 us
    scatter x16, local copies, waits for them, and re-layouts, advance_wide(): return state.at[:, 1:-1].set(updated)  42.5 us
    another operation x3, other arithmetic, body(): jax.scipy.linalg.cho_solve((factor, True), target)  39.4 us
    ppermute x2, waiting for transfers between devices, collected_by_bits(): theirs = lax.ppermute(parts, axis, [(i, i ^ bit) for i in range(length)])  32.8 us
    another operation x17, other arithmetic  21.6 us
    gather x1, local copies, waits for them, and re-layouts, body(): obs_mean = jnp.take(realization_average, slot_cell_index)  17.4 us
    psum x1, blocking collectives, body(): lax.psum(jnp.sum(predicted_traffic_load, axis=0), 'member')  16.3 us
    min x16, other arithmetic, advance_wide(): fluxes = jnp.minimum(demand[:, :-1], supply[:, 1:])  15.8 us
  transfers between devices with their start and end apart: 10, of which 5 were waited for; matrix products, arithmetic and copies ran while one was open for 65% of the time, Pallas kernels for 0%

profile of v1, /device:TPU:0, one launch (start us, length us, event | category | flops | bytes accessed | tf_op | source)
XLA Modules:
  0.0 381.2 jit_solution(1705997889292946786)
XLA Ops:
  8.4 4.9 %collective-permute-start.2 = (f32[4,16]{1,0:T(4,128)S(1)}, f32[4,16]{1,0:T(4,128)S(1)}, u32[]{:S(2)}, u32[]{:S(2)}) collective-permute-start(f32[4,16]{1,0:T(4,128)S(1)} %get-tuple-element.210), channel_id=1, source_target_pairs={{0,1},{1,2},{2,3},{3,4},{4,5},{5,6},{6,7},{8,9},{9,10},{10,11},{11... | collective-permute-start | bytes 776 | tf_op jit(solution)/shard_map/ppermute | solution.py:41
  15.5 4.5 %collective-permute-start = (f32[32,16]{1,0:T(8,128)S(1)}, f32[32,16]{1,0:T(8,128)S(1)}, u32[]{:S(2)}, u32[]{:S(2)}) collective-permute-start(f32[32,16]{1,0:T(8,128)S(1)} %get-tuple-element.204), channel_id=1, source_target_pairs={{0,1},{1,2},{2,3},{3,4},{4,5},{5,6},{6,7},{8,9},{9,10},{10,11},{11... | collective-permute-start | bytes 6152 | tf_op jit(solution)/shard_map/ppermute | solution.py:41
  26.4 90.7 %while.15 = (s32[]{:T(128)}, f32[32,8224]{1,0:T(8,128)S(1)}, pred[]{:T(512)}, f32[1,8224]{1,0:T(1,128)S(1)}, f32[1,8224]{1,0:T(1,128)S(1)}, /*index=5*/f32[]{:T(...) while((s32[]{:T(128)}, f32[32,8224]{1,0:T(8,128)S(1)}, ...), condition=%wide.region_2.3_spmd.clone, body=%wide.region_1.0_spmd.clone.sunk | while | flops 2647714 | bytes 10195928 | solution.py:98
  28.1 1.3 fusion.64
  29.4 2.7 scatter.7
  35.1 2.7 scatter.7
  40.8 2.7 scatter.7
  46.4 2.7 scatter.7
  52.1 2.7 scatter.7
  57.8 2.7 scatter.7
  63.4 2.7 scatter.7
  69.1 2.7 scatter.7
  74.8 2.7 scatter.7
  80.4 2.7 scatter.7
  86.1 2.7 scatter.7
  91.8 2.7 scatter.7
  97.4 2.7 scatter.7
  103.1 2.7 scatter.7
  108.8 2.7 scatter.7
  114.5 2.7 scatter.7
  117.5 16.3 %psum.21 = f32[8192]{0:T(1024)S(1)} all-reduce(f32[8192]{0:T(1024)S(1)} %slice_reduce_fusion), channel_id=1, replica_groups=mesh['member'=4,'region'=2,'block'=4] {'member'}, use_global_device_ids=true, to_apply=%region_4.5 | all-reduce | flops 8192 | bytes 65536 | tf_op jit(solution)/shard_map/psum | solution.py:101
  134.1 2.7 copy.79
  136.8 17.4 %gather_fusion = f32[3072]{0:T(1024)S(1)} fusion(f32[8192]{0:T(1024)S(1)} %broadcast_multiply_fusion.1, s32[3072]{0:T(1024)S(1)} %broadcast_clamp_fusion), kind=kCustom, calls=%fused_computation | custom fusion | bytes 36864 | tf_op jit(solution)/shard_map/jit(_take)/gather | solution.py:108
  154.3 10.3 %gather_fusion.1 = f32[3072,32]{1,0:T(8,128)S(1)} fusion(f32[32,8192]{0,1:T(8,128)} %copy.79, s32[3072]{0:T(1024)S(1)} %broadcast_clamp_fusion), kind=kCustom, calls=%fused_computation.1 | custom fusion | bytes 798720 | tf_op jit(solution)/shard_map/jit(_take)/gather | solution.py:107
  165.3 2.5 bitcast_select_fusion
  167.8 1.8 copy.80
  169.7 2.5 bitcast_select_fusion.1
  172.2 8.0 %collective-permute-done.4 = f32[1,32,3072]{2,1,0:T(8,128)S(1)} collective-permute-done((f32[1,32,3072]{2,1,0:T(8,128)S(1)}, f32[1,32,3072]{2,1,0:T(8,128)S(1)}, u32[]{:S(2)}, u32[]{:S(2)}) %collective-permute-start.4) | collective-permute-done | bytes 393248 | tf_op jit(solution)/shard_map/ppermute | solution.py:23
  180.2 1.6 copy.81
  181.8 1.6 pad_maximum_fusion
  183.4 3.0 fusion.10
  186.4 2.3 copy.82
  189.8 2.3 copy.83
  192.1 24.7 %collective-permute-done.5 = f32[2,32,3072]{2,1,0:T(8,128)S(1)} collective-permute-done((f32[2,32,3072]{2,1,0:T(8,128)S(1)}, f32[2,32,3072]{2,1,0:T(8,128)S(1)}, u32[]{:S(2)}, u32[]{:S(2)}) %collective-permute-start.5) | collective-permute-done | bytes 786464 | tf_op jit(solution)/shard_map/ppermute | solution.py:23
  219.8 14.5 %all-reduce = (f32[]{:T(128)}, f32[]{:T(128)}) all-reduce(f32[]{:T(128)} %get-tuple-element.193, f32[]{:T(128)} %select_reduce_fusion.1), channel_id=1, replica_groups=mesh['member'=4,'region'=2,'block'=4] {'region','block'}, use_global_device_ids=true, to_apply=%region_6.7 | all-reduce | flops 2 | bytes 16 | tf_op jit(solution)/shard_map/psum | solution.py:121
  235.6 1.4 fusion.19
  237.0 2.1 mul.159
  241.4 3.4 fusion.20
  244.9 1.8 bitcast_subtract_fusion
  246.8 1.7 fusion.25
  248.5 4.2 %collective-permute-start.6 = (f32[2,4,128,128]{3,2,1,0:T(8,128)S(1)}, f32[2,4,128,128]{3,2,1,0:T(8,128)S(1)}, u32[]{:S(2)}, u32[]{:S(2)}) collective-permute-start(f32[2,4,128,128]{3,2,1,0:T(8,128)S(1)} %pad_maximum_fusion.3), channel_id=1, source_target_pairs={{0,1},{1,2},{2,3},{3,4},{4,5},{5,6},{6,7},{8,9},{9,10},{10,11},{11... | collective-permute-start | bytes 1572872 | tf_op jit(solution)/shard_map/ppermute | solution.py:41
  254.3 10.7 %collective-permute-done.6 = f32[2,4,128,128]{3,2,1,0:T(8,128)S(1)} collective-permute-done((f32[2,4,128,128]{3,2,1,0:T(8,128)S(1)}, f32[2,4,128,128]{3,2,1,0:T(8,128)S(1)}, u32[]{:S(2)}, u32[]{:S(2)}) %collective-permute-start.6) | collective-permute-done | bytes 524320 | tf_op jit(solution)/shard_map/ppermute | solution.py:41
  265.0 6.0 %collective-permute-done.7 = f32[2,4,128,128]{3,2,1,0:T(8,128)S(1)} collective-permute-done((f32[2,4,128,128]{3,2,1,0:T(8,128)S(1)}, f32[2,4,128,128]{3,2,1,0:T(8,128)S(1)}, u32[]{:S(2)}, u32[]{:S(2)}) %collective-permute-start.7) | collective-permute-done | bytes 524320 | tf_op jit(solution)/shard_map/ppermute | solution.py:42
  272.6 46.9 %custom-call.11 = f32[4,128,128]{2,1,0:T(8,128)S(1)} custom-call(f32[4,128,128]{2,1,0:T(8,128)S(1)} %fusion.39), custom_call_target="Cholesky" | custom-call | tf_op jit(solution)/shard_map/jit(cholesky)/cholesky | solution.py:152
  319.8 39.3 %custom-call.12 = f32[4,1,128,128]{2,3,1,0:T(8,128)S(1)} custom-call(f32[4,1,128,128]{3,2,1,0:T(8,128)S(1)} %select_bitcast_fusion), custom_call_target="InvertDiagBlocksLowerTriangular" | custom-call | tf_op jit(solution)/shard_map/vmap(jit(_cho_solve))/triangular_solve | solution.py:153
  361.4 5.6 %copy.97 = f32[128,8192]{0,1:T(8,128)} copy(f32[128,8192]{1,0:T(8,128)} %all-gather.5.cloned.1.call-done) | data formatting | bytes 8388608 | tf_op jit(solution)/shard_map/all_gather | solution.py:158
  367.0 6.0 %fusion.11 = f32[4,4,8,2048]{3,2,1,0:T(8,128)S(1)} fusion(f32[128,4,2048]{0,2,1:T(8,128)} %bitcast.67, f32[]{:T(128)S(6)} %sqrt.6, f32[4,128,128]{1,2,0:T(8,128)S(1)} %fusion.34, s32[]{:T(128)S(6)} %select_n.75), kind=kOutput, calls=%fused_computation.20 | convolution fusion | flops 402915328 | bytes 5308424 | tf_op jit(solution)/shard_map/kbc,bkj->jbc/dot_general | solution.py:163
  373.1 1.3 add_add_fusion
  (255 shorter events, 69.6 us)
Async XLA Ops:
  6.5 19.2 %copy-start.6 = (f32[32,8192]{1,0:T(8,128)S(1)}, f32[32,8192]{1,0:T(8,128)}, u32[]{:S(2)}) copy-start(f32[32,8192]{1,0:T(8,128)} %param.15) | copy-start | bytes 3145732
  6.5 238.3 %all-gather.3.cloned.1.call-start = ((), (), s32[]{:S(2)}) async-start(), calls=%async_computation | async-start | bytes 1966080 | tf_op jit(solution)/shard_map/all_gather | solution.py:118
  8.4 15.8 %collective-permute-start.2 = (f32[4,16]{1,0:T(4,128)S(1)}, f32[4,16]{1,0:T(4,128)S(1)}, u32[]{:S(2)}, u32[]{:S(2)}) collective-permute-start(f32[4,16]{1,0:T(4,128)S(1)} %get-tuple-element.210), channel_id=1, source_target_pairs={{0,1},{1,2},{2,3},{3,4},{4,5},{5,6},{6,7},{8,9},{9,10},{10,11},{11... | collective-permute-start | bytes 776 | tf_op jit(solution)/shard_map/ppermute | solution.py:41
  13.4 10.8 %collective-permute-start.3 = (f32[4,16]{1,0:T(4,128)S(1)}, f32[4,16]{1,0:T(4,128)S(1)}, u32[]{:S(2)}, u32[]{:S(2)}) collective-permute-start(f32[4,16]{1,0:T(4,128)S(1)} %get-tuple-element.209), channel_id=1, source_target_pairs={{1,0},{2,1},{3,2},{4,3},{5,4},{6,5},{7,6},{9,8},{10,9},{11,10},{12... | collective-permute-start | bytes 776 | tf_op jit(solution)/shard_map/ppermute | solution.py:42
  15.5 9.0 %collective-permute-start = (f32[32,16]{1,0:T(8,128)S(1)}, f32[32,16]{1,0:T(8,128)S(1)}, u32[]{:S(2)}, u32[]{:S(2)}) collective-permute-start(f32[32,16]{1,0:T(8,128)S(1)} %get-tuple-element.204), channel_id=1, source_target_pairs={{0,1},{1,2},{2,3},{3,4},{4,5},{5,6},{6,7},{8,9},{9,10},{10,11},{11... | collective-permute-start | bytes 6152 | tf_op jit(solution)/shard_map/ppermute | solution.py:41
  20.1 5.6 %collective-permute-start.1 = (f32[32,16]{1,0:T(8,128)S(1)}, f32[32,16]{1,0:T(8,128)S(1)}, u32[]{:S(2)}, u32[]{:S(2)}) collective-permute-start(f32[32,16]{1,0:T(8,128)S(1)} %get-tuple-element.203), channel_id=1, source_target_pairs={{1,0},{2,1},{3,2},{4,3},{5,4},{6,5},{7,6},{9,8},{10,9},{11,10},{12... | collective-permute-start | bytes 6152 | tf_op jit(solution)/shard_map/ppermute | solution.py:42
  21.4 340.0 %all-gather.5.cloned.1.call-start = ((), (), s32[]{:S(2)}) async-start(), calls=%async_computation.1 | async-start | bytes 5242880 | tf_op jit(solution)/shard_map/all_gather | solution.py:158
  134.1 2.7 copy-start.4
  154.2 10.4 %copy-start.8 = (f32[3072]{0:T(1024)S(1)}, f32[3072]{0:T(1024)}, u32[]{:S(2)}) copy-start(f32[3072]{0:T(1024)} %param.23) | copy-start | bytes 36868
  154.3 10.4 %copy-start.9 = (s32[3072]{0:T(1024)S(1)}, s32[3072]{0:T(1024)}, u32[]{:S(2)}) copy-start(s32[3072]{0:T(1024)} %param.20) | copy-start | bytes 36868
  154.3 10.4 %copy-start.10 = (f32[3072]{0:T(1024)S(1)}, f32[3072]{0:T(1024)}, u32[]{:S(2)}) copy-start(f32[3072]{0:T(1024)} %param.22) | copy-start | bytes 36868
  169.6 10.6 %collective-permute-start.4 = (f32[1,32,3072]{2,1,0:T(8,128)S(1)}, f32[1,32,3072]{2,1,0:T(8,128)S(1)}, u32[]{:S(2)}, u32[]{:S(2)}) collective-permute-start(f32[1,32,3072]{2,1,0:T(8,128)S(1)} %copy.80), channel_id=1, source_target_pairs={{0,8},{8,0},{16,24},{24,16},{1,9},{9,1},{17,25},{25,17},{2,10},{10... | collective-permute-start | bytes 1179656 | tf_op jit(solution)/shard_map/ppermute | solution.py:23
  172.2 9.7 %copy-start.5 = (f32[1,1,32,3072]{2,3,1,0:T(8,128)S(1)}, f32[1,1,32,3072]{2,3,1,0:T(8,128)}, u32[]{:S(2)}) copy-start(f32[1,1,32,3072]{2,3,1,0:T(8,128)} %bitcast_select_fusion.1) | copy-start | bytes 1179652
  188.8 28.1 %collective-permute-start.5 = (f32[2,32,3072]{2,1,0:T(8,128)S(1)}, f32[2,32,3072]{2,1,0:T(8,128)S(1)}, u32[]{:S(2)}, u32[]{:S(2)}) collective-permute-start(f32[2,32,3072]{2,1,0:T(8,128)S(1)} %copy.82), channel_id=1, source_target_pairs={{0,16},{8,24},{16,0},{24,8},{1,17},{9,25},{17,1},{25,9},{2,18},{10... | collective-permute-start | bytes 2359304 | tf_op jit(solution)/shard_map/ppermute | solution.py:23
  216.8 0.9 copy-start.7
  239.0 1.2 copy-start.1
  240.2 1.2 copy-start.2
  241.4 3.5 copy-start
  244.9 1.9 copy-start.3
  246.8 7.3 %copy-start.11 = (s32[4,3]{1,0:T(4,128)S(1)}, s32[4,3]{1,0:T(4,128)}, u32[]{:S(2)}) copy-start(s32[4,3]{1,0:T(4,128)} %param.25) | copy-start | bytes 148
  248.5 16.5 %collective-permute-start.6 = (f32[2,4,128,128]{3,2,1,0:T(8,128)S(1)}, f32[2,4,128,128]{3,2,1,0:T(8,128)S(1)}, u32[]{:S(2)}, u32[]{:S(2)}) collective-permute-start(f32[2,4,128,128]{3,2,1,0:T(8,128)S(1)} %pad_maximum_fusion.3), channel_id=1, source_target_pairs={{0,1},{1,2},{2,3},{3,4},{4,5},{5,6},{6,7},{8,9},{9,10},{10,11},{11... | collective-permute-start | bytes 1572872 | tf_op jit(solution)/shard_map/ppermute | solution.py:41
  252.7 18.3 %collective-permute-start.7 = (f32[2,4,128,128]{3,2,1,0:T(8,128)S(1)}, f32[2,4,128,128]{3,2,1,0:T(8,128)S(1)}, u32[]{:S(2)}, u32[]{:S(2)}) collective-permute-start(f32[2,4,128,128]{3,2,1,0:T(8,128)S(1)} %pad_maximum_fusion.3), channel_id=1, source_target_pairs={{1,0},{2,1},{3,2},{4,3},{5,4},{6,5},{7,6},{9,8},{10,9},{11,10},{12... | collective-permute-start | bytes 1572872 | tf_op jit(solution)/shard_map/ppermute | solution.py:42
Sparse Core Ops, SparseCore 0:
  21.5 33.1 all-gather.2
  189.9 55.5 all-gather.4
